TPU v7x, 32 devices: a whole 2x2x4 slice. The times are simulated.
32 devices in a mesh: blk: 8 (over z, x), grp: 4 (over y, core).
Axes of the slice: x: 2, y: 2, z: 4, core: 2. Of those that a mesh axis runs over, the one named last changes fastest.
Arguments:
- source_coords: float32 [3, 20480], P(None, ('blk', 'grp')), may hold values from 0 to 8, as said below
- source_values: float32 [3, 20480], P(None, ('blk', 'grp')), may hold values from -48 to 48
- target_coords: float32 [3, 16384], P(None, ('blk', 'grp')), may hold values from 0 to 8, as said below
- target_owner: int32 [16384], P(('blk', 'grp')), may hold values from 0 to 7, as said below
Outputs:
- weights: float32 [3, 20480], P(None, ('blk', 'grp'))
- poly: float32 [3, 4], replicated
- mapped: float32 [3, 16384], P(None, ('blk', 'grp'))
Inputs may be any that keep to these rules, and one draw needn't show every extreme that they name: `source_coords`: source vertex j has its first coordinate between j // 2560 and j // 2560 + 1, and the other two between 0 and 1. `target_coords`: target vertex t has its first coordinate between target_owner[t] and target_owner[t] + 1, and the other two between 0 and 1. target_owner[t] differs from t // 2048 by at most one.
All inputs are finite; a program needn't handle non-finite values.
Results may differ from a plain program's by a relative error of at most 0.0003.
Values sent between devices are 32-bit elements; how exact they have to be, the bound alone decides.
A program may use at most 64 MiB of HBM per device.

v0:
```python
import math

import jax
import jax.numpy as jnp
from jax import lax
from jax.sharding import PartitionSpec as P

ITERS = 3
REACH = 2


precise = lax.Precision.HIGHEST
thin_factor = 0.6
tiny = 1e-06


def from_behind(value, axis, steps):
    count = lax.axis_size(axis)
    initial, last = (max(0, -steps), min(count, count - steps))
    return lax.ppermute(value, axis, [(source, source + steps) for source in range(initial, last)])


def kernel_tile(rows, cols, stretch):
    along = rows[0][None, :] - cols[0][:, None]
    across = rows[1][None, :] - cols[1][:, None]
    upward = rows[2][None, :] - cols[2][:, None]
    return jnp.exp(-(thin_factor * along * along + stretch * (across * across + upward * upward)))


def basis(points, partitions, sources):
    ones = jnp.ones_like(points[0])
    stacked = jnp.stack(
        [ones, 2.0 * points[0] / partitions - 1.0, 2.0 * points[1] - 1.0, 2.0 * points[2] - 1.0]
    )
    return stacked / math.sqrt(sources)


def least_squares(hessenberg, beta):
    count = len(hessenberg)
    right_side = [beta] + [jnp.zeros_like(beta) for k in range(count)]
    upper = []
    cosines = []
    sines = []
    for k in range(count):
        column = list(hessenberg[k])
        for i in range(k):
            top = cosines[i] * column[i] + sines[i] * column[i + 1]
            lower = -sines[i] * column[i] + cosines[i] * column[i + 1]
            column[i] = top
            column[i + 1] = lower
        radius = jnp.sqrt(column[k] * column[k] + column[k + 1] * column[k + 1])
        cosine = column[k] / radius
        sine = column[k + 1] / radius
        column[k] = radius
        cosines.append(cosine)
        sines.append(sine)
        right_side[k + 1] = -sine * right_side[k]
        right_side[k] = cosine * right_side[k]
        upper.append(column[: k + 1])
    solved = [None] * count
    for k in reversed(range(count)):
        running = right_side[k]
        for j in range(k + 1, count):
            running = running - upper[j][k] * solved[j]
        solved[k] = running / upper[k][k]
    return solved


def near_slabs(block, reach):
    slab = lax.all_gather(block, "grp", axis=1, tiled=True)
    pieces = []
    for offset in range(-reach, reach + 1):
        if offset == 0:
            pieces.append(slab)
        else:
            pieces.append(from_behind(slab, "blk", -offset))
    return jnp.stack(pieces)


def apply_near(rows, near_coords, near_values, owners, first_slab, stretch, reach):
    labels = jnp.arange(near_coords.shape[0], dtype=jnp.int32) + first_slab

    def add_slab(running, item):
        cols, values, slab = item
        tile = kernel_tile(rows, cols, stretch)
        if owners is not None:
            tile = jnp.where((jnp.abs(owners - slab) <= reach)[None, :], tile, 0.0)
        return (
            running + jnp.dot(values, tile, precision=precise, preferred_element_type=jnp.float32),
            None,
        )

    start = jnp.zeros((near_values.shape[1], rows.shape[1]), jnp.float32)
    result, unused = lax.scan(add_slab, start, (near_coords, near_values, labels))
    return result


def shards(source_coords, source_values, target_coords, target_owner):
    reach = REACH
    own_rows = source_coords.shape[1]
    slab_len = own_rows * lax.axis_size("grp")
    partitions = lax.axis_size("blk")
    sources = slab_len * partitions
    stretch = 4.0 * slab_len
    here = lax.axis_index("blk")
    poly_src = basis(source_coords, partitions, sources)
    start_sq, start_moment = lax.psum(
        (
            jnp.sum(source_values * source_values, axis=1),
            jnp.dot(
                source_values, poly_src.T, precision=precise, preferred_element_type=jnp.float32
            ),
        ),
        ("blk", "grp"),
    )
    beta = jnp.sqrt(start_sq + tiny)
    heads = [source_values / beta[:, None]]
    tails = [jnp.zeros_like(start_moment)]
    moments = [start_moment / beta[:, None]]
    hessenberg = []
    for k in range(ITERS):
        both_near = near_slabs(jnp.concatenate([source_coords, heads[k]], axis=0), reach)
        cols = both_near[:, :3]
        values_near = both_near[:, 3:]
        image_head = apply_near(
            source_coords, cols, values_near, None, here - reach, stretch, reach
        ) + jnp.dot(tails[k], poly_src, precision=precise, preferred_element_type=jnp.float32)
        image_tail = moments[k]
        column = []
        local_dots = jnp.stack(
            [jnp.sum(heads[i] * image_head, axis=1) for i in range(k + 1)], axis=1
        )
        head_dots, image_sq, image_moment = lax.psum(
            (
                local_dots,
                jnp.sum(image_head * image_head, axis=1),
                jnp.dot(
                    image_head, poly_src.T, precision=precise, preferred_element_type=jnp.float32
                ),
            ),
            ("blk", "grp"),
        )
        full_sq = image_sq + jnp.sum(image_tail * image_tail, axis=1)
        rest_head = image_head
        rest_tail = image_tail
        rest_moment = image_moment
        for i in range(k + 1):
            factor = head_dots[:, i] + jnp.sum(tails[i] * image_tail, axis=1)
            full_sq = full_sq - factor * factor
            rest_head = rest_head - factor[:, None] * heads[i]
            rest_tail = rest_tail - factor[:, None] * tails[i]
            rest_moment = rest_moment - factor[:, None] * moments[i]
            column.append(factor)
        length = jnp.sqrt(full_sq + tiny)
        column.append(length)
        hessenberg.append(column)
        heads.append(rest_head / length[:, None])
        tails.append(rest_tail / length[:, None])
        moments.append(rest_moment / length[:, None])
    solved = least_squares(hessenberg, beta)
    weights = solved[0][:, None] * heads[0]
    poly = solved[0][:, None] * tails[0]
    for k in range(1, ITERS):
        weights = weights + solved[k][:, None] * heads[k]
        poly = poly + solved[k][:, None] * tails[k]
    joined_near = near_slabs(jnp.concatenate([source_coords, weights], axis=0), reach + 1)
    cols_far = joined_near[:, :3]
    weights_near = joined_near[:, 3:]
    poly_tgt = basis(target_coords, partitions, sources)
    mapped = apply_near(
        target_coords, cols_far, weights_near, target_owner, here - reach - 1, stretch, reach
    )
    mapped = mapped + jnp.dot(poly, poly_tgt, precision=precise, preferred_element_type=jnp.float32)
    return (weights, poly, mapped)


def solution(mesh):
    return jax.shard_map(
        shards,
        mesh=mesh,
        in_specs=(
            P(None, ("blk", "grp")),
            P(None, ("blk", "grp")),
            P(None, ("blk", "grp")),
            P(("blk", "grp")),
        ),
        out_specs=(P(None, ("blk", "grp")), P(), P(None, ("blk", "grp"))),
        check_vma=False,
    )
```

profile of v0, /device:TPU:0, one launch (start us, length us, event | category | flops | bytes accessed | tf_op | source)
XLA Modules:
  0.0 391.3 jit_solution(17570499681100357009)
XLA Ops:
  1.5 42.0 %psum.70 = f32[3]{0:T(128)S(1)} all-reduce(f32[3]{0:T(128)S(1)} %multiply_reduce_fusion.9), channel_id=1, replica_groups=mesh['blk'=8,'grp'=4] {'blk','grp'}, use_global_device_ids=true, to_apply=%region_1.0 | all-reduce | flops 3 | bytes 24 | tf_op jit(solution)/shard_map/psum | solution.py:107
  44.9 5.5 %all_gather.12 = f32[6,2560]{1,0:T(8,128)S(1)} all-gather(f32[6,640]{1,0:T(8,128)S(1)} %pad_maximum_fusion.3), channel_id=1, replica_groups=mesh['blk'=8,'grp'=4] {'grp'}, dimensions={1}, use_global_device_ids=true | all-gather | bytes 76800 | tf_op jit(solution)/shard_map/all_gather | solution.py:70
  66.5 29.7 %while.44 = (s32[]{:T(128)}, f32[3,640]{1,0:T(4,128)S(1)}, f32[5,3,2560]{2,1,0:T(4,128)S(1)}, f32[3,640]{1,0:T(4,128)S(1)}, f32[5,3,2560]{2,1,0:T(4,128)S(1)}, /*index=5*/s32[]{:T(128)}, s32[]{:T(128)}, s32[]{}, s32[]{}) while((s32[]{:T(128)}, f32[3,640]{1,0:T(4,128)S(1)}, f32[5,3,2560]{2,1,0:T(4,128)S(1)}, ...), condition=%wide.region_3.4_spmd.clone, body=%wide.region_2.0_spmd.clone.sunk | while | flops 77008640 | bytes 184975 | solution.py:94
  66.6 5.8 %fusion.163 = f32[3,640]{1,0:T(4,128)S(1)} fusion(f32[2560]{0:T(1024)S(1)} %get-tuple-element.469, f32[640]{0:T(1024)S(1)} %get-tuple-element.470, f32[2560]{0:T(1024)S(1)} %get-tuple-element.471, f32[640]{0:T(1024)S(1)} %get-tuple-element.472, f32[2560]{0:T(1024)S(1)} %get-tuple-element.473, f32[640]{0:T(1024)S(1)} %get-tuple-element.474, ...), kind=kOutput, calls=%fused_computation.20.clone.1 | convolution fusion | flops 77008640 | bytes 108037 | tf_op jit(solution)/shard_map/while/body/eval_jaxpr/dot_general | solution.py:89
  72.5 5.8 %fusion.163 = f32[3,640]{1,0:T(4,128)S(1)} fusion(f32[2560]{0:T(1024)S(1)} %get-tuple-element.469, f32[640]{0:T(1024)S(1)} %get-tuple-element.470, f32[2560]{0:T(1024)S(1)} %get-tuple-element.471, f32[640]{0:T(1024)S(1)} %get-tuple-element.472, f32[2560]{0:T(1024)S(1)} %get-tuple-element.473, f32[640]{0:T(1024)S(1)} %get-tuple-element.474, ...), kind=kOutput, calls=%fused_computation.20.clone.1 | convolution fusion | flops 77008640 | bytes 108037 | tf_op jit(solution)/shard_map/while/body/eval_jaxpr/dot_general | solution.py:89
  78.5 5.8 %fusion.163 = f32[3,640]{1,0:T(4,128)S(1)} fusion(f32[2560]{0:T(1024)S(1)} %get-tuple-element.469, f32[640]{0:T(1024)S(1)} %get-tuple-element.470, f32[2560]{0:T(1024)S(1)} %get-tuple-element.471, f32[640]{0:T(1024)S(1)} %get-tuple-element.472, f32[2560]{0:T(1024)S(1)} %get-tuple-element.473, f32[640]{0:T(1024)S(1)} %get-tuple-element.474, ...), kind=kOutput, calls=%fused_computation.20.clone.1 | convolution fusion | flops 77008640 | bytes 108037 | tf_op jit(solution)/shard_map/while/body/eval_jaxpr/dot_general | solution.py:89
  84.4 5.8 %fusion.163 = f32[3,640]{1,0:T(4,128)S(1)} fusion(f32[2560]{0:T(1024)S(1)} %get-tuple-element.469, f32[640]{0:T(1024)S(1)} %get-tuple-element.470, f32[2560]{0:T(1024)S(1)} %get-tuple-element.471, f32[640]{0:T(1024)S(1)} %get-tuple-element.472, f32[2560]{0:T(1024)S(1)} %get-tuple-element.473, f32[640]{0:T(1024)S(1)} %get-tuple-element.474, ...), kind=kOutput, calls=%fused_computation.20.clone.1 | convolution fusion | flops 77008640 | bytes 108037 | tf_op jit(solution)/shard_map/while/body/eval_jaxpr/dot_general | solution.py:89
  90.4 5.8 %fusion.163 = f32[3,640]{1,0:T(4,128)S(1)} fusion(f32[2560]{0:T(1024)S(1)} %get-tuple-element.469, f32[640]{0:T(1024)S(1)} %get-tuple-element.470, f32[2560]{0:T(1024)S(1)} %get-tuple-element.471, f32[640]{0:T(1024)S(1)} %get-tuple-element.472, f32[2560]{0:T(1024)S(1)} %get-tuple-element.473, f32[640]{0:T(1024)S(1)} %get-tuple-element.474, ...), kind=kOutput, calls=%fused_computation.20.clone.1 | convolution fusion | flops 77008640 | bytes 108037 | tf_op jit(solution)/shard_map/while/body/eval_jaxpr/dot_general | solution.py:89
  96.5 40.0 %all-reduce.2 = (f32[3]{0:T(128)S(1)}, f32[3,4]{1,0:T(4,128)S(1)}, f32[3,1]{0,1:T(1,128)S(1)}) all-reduce(f32[3]{0:T(128)S(1)} %get-tuple-element.232, f32[3,4]{1,0:T(4,128)S(1)} %convolution_bitcast_fusion, f32[3,1]{0,1:T(1,128)S(1)} %bitcast.208), channel_id=1, replica_groups=mesh['blk'=8,'grp'=4] {'blk','grp'}, use_global_device_ids=true, to_apply=%region_9.10 | all-reduce | flops 18 | bytes 144 | tf_op jit(solution)/shard_map/psum | solution.py:133
  136.8 5.5 %all_gather.13 = f32[6,2560]{1,0:T(8,128)S(1)} all-gather(f32[6,640]{1,0:T(8,128)S(1)} %pad_maximum_fusion.2), channel_id=1, replica_groups=mesh['blk'=8,'grp'=4] {'grp'}, dimensions={1}, use_global_device_ids=true | all-gather | bytes 76800 | tf_op jit(solution)/shard_map/all_gather | solution.py:70
  156.6 29.7 %while.45 = (s32[]{:T(128)}, f32[3,640]{1,0:T(4,128)S(1)}, f32[5,3,2560]{2,1,0:T(4,128)S(1)}, f32[3,640]{1,0:T(4,128)S(1)}, f32[5,3,2560]{2,1,0:T(4,128)S(1)}, /*index=5*/s32[]{:T(128)}, s32[]{:T(128)}, s32[]{}, s32[]{}) while((s32[]{:T(128)}, f32[3,640]{1,0:T(4,128)S(1)}, f32[5,3,2560]{2,1,0:T(4,128)S(1)}, ...), condition=%wide.region_12.13_spmd.clone, body=%wide.region_11.12_spmd.clone.sunk | while | flops 77008640 | bytes 184975 | solution.py:94
  156.8 5.8 %fusion.166 = f32[3,640]{1,0:T(4,128)S(1)} fusion(f32[2560]{0:T(1024)S(1)} %get-tuple-element.480, f32[640]{0:T(1024)S(1)} %get-tuple-element.481, f32[2560]{0:T(1024)S(1)} %get-tuple-element.482, f32[640]{0:T(1024)S(1)} %get-tuple-element.483, f32[2560]{0:T(1024)S(1)} %get-tuple-element.484, f32[640]{0:T(1024)S(1)} %get-tuple-element.485, ...), kind=kOutput, calls=%fused_computation.52.clone.1 | convolution fusion | flops 77008640 | bytes 108037 | tf_op jit(solution)/shard_map/while/body/eval_jaxpr/dot_general | solution.py:89
  162.7 5.8 %fusion.166 = f32[3,640]{1,0:T(4,128)S(1)} fusion(f32[2560]{0:T(1024)S(1)} %get-tuple-element.480, f32[640]{0:T(1024)S(1)} %get-tuple-element.481, f32[2560]{0:T(1024)S(1)} %get-tuple-element.482, f32[640]{0:T(1024)S(1)} %get-tuple-element.483, f32[2560]{0:T(1024)S(1)} %get-tuple-element.484, f32[640]{0:T(1024)S(1)} %get-tuple-element.485, ...), kind=kOutput, calls=%fused_computation.52.clone.1 | convolution fusion | flops 77008640 | bytes 108037 | tf_op jit(solution)/shard_map/while/body/eval_jaxpr/dot_general | solution.py:89
  168.6 5.8 %fusion.166 = f32[3,640]{1,0:T(4,128)S(1)} fusion(f32[2560]{0:T(1024)S(1)} %get-tuple-element.480, f32[640]{0:T(1024)S(1)} %get-tuple-element.481, f32[2560]{0:T(1024)S(1)} %get-tuple-element.482, f32[640]{0:T(1024)S(1)} %get-tuple-element.483, f32[2560]{0:T(1024)S(1)} %get-tuple-element.484, f32[640]{0:T(1024)S(1)} %get-tuple-element.485, ...), kind=kOutput, calls=%fused_computation.52.clone.1 | convolution fusion | flops 77008640 | bytes 108037 | tf_op jit(solution)/shard_map/while/body/eval_jaxpr/dot_general | solution.py:89
  174.6 5.8 %fusion.166 = f32[3,640]{1,0:T(4,128)S(1)} fusion(f32[2560]{0:T(1024)S(1)} %get-tuple-element.480, f32[640]{0:T(1024)S(1)} %get-tuple-element.481, f32[2560]{0:T(1024)S(1)} %get-tuple-element.482, f32[640]{0:T(1024)S(1)} %get-tuple-element.483, f32[2560]{0:T(1024)S(1)} %get-tuple-element.484, f32[640]{0:T(1024)S(1)} %get-tuple-element.485, ...), kind=kOutput, calls=%fused_computation.52.clone.1 | convolution fusion | flops 77008640 | bytes 108037 | tf_op jit(solution)/shard_map/while/body/eval_jaxpr/dot_general | solution.py:89
  180.5 5.8 %fusion.166 = f32[3,640]{1,0:T(4,128)S(1)} fusion(f32[2560]{0:T(1024)S(1)} %get-tuple-element.480, f32[640]{0:T(1024)S(1)} %get-tuple-element.481, f32[2560]{0:T(1024)S(1)} %get-tuple-element.482, f32[640]{0:T(1024)S(1)} %get-tuple-element.483, f32[2560]{0:T(1024)S(1)} %get-tuple-element.484, f32[640]{0:T(1024)S(1)} %get-tuple-element.485, ...), kind=kOutput, calls=%fused_computation.52.clone.1 | convolution fusion | flops 77008640 | bytes 108037 | tf_op jit(solution)/shard_map/while/body/eval_jaxpr/dot_general | solution.py:89
  186.7 41.0 %all-reduce.1 = (f32[3]{0:T(128)S(1)}, f32[3,4]{1,0:T(4,128)S(1)}, f32[3,2]{0,1:T(2,128)S(1)}) all-reduce(f32[3]{0:T(128)S(1)} %get-tuple-element.229, f32[3,4]{1,0:T(4,128)S(1)} %fusion.135, f32[3,2]{0,1:T(2,128)S(1)} %pad_maximum_fusion.5), channel_id=1, replica_groups=mesh['blk'=8,'grp'=4] {'blk','grp'}, use_global_device_ids=true, to_apply=%region_20.21 | all-reduce | flops 21 | bytes 168 | tf_op jit(solution)/shard_map/psum | solution.py:133
  228.1 5.5 %all_gather.14 = f32[6,2560]{1,0:T(8,128)S(1)} all-gather(f32[6,640]{1,0:T(8,128)S(1)} %pad_maximum_fusion.1), channel_id=1, replica_groups=mesh['blk'=8,'grp'=4] {'grp'}, dimensions={1}, use_global_device_ids=true | all-gather | bytes 76800 | tf_op jit(solution)/shard_map/all_gather | solution.py:70
  248.0 29.7 %while.46 = (s32[]{:T(128)}, f32[3,640]{1,0:T(4,128)S(1)}, f32[5,3,2560]{2,1,0:T(4,128)S(1)}, f32[3,640]{1,0:T(4,128)S(1)}, f32[5,3,2560]{2,1,0:T(4,128)S(1)}, /*index=5*/s32[]{:T(128)}, s32[]{:T(128)}, s32[]{}, s32[]{}) while((s32[]{:T(128)}, f32[3,640]{1,0:T(4,128)S(1)}, f32[5,3,2560]{2,1,0:T(4,128)S(1)}, ...), condition=%wide.region_23.24_spmd.clone, body=%wide.region_22.23_spmd.clone.sunk | while | flops 77008640 | bytes 184975 | solution.py:94
  248.1 5.8 %fusion.169 = f32[3,640]{1,0:T(4,128)S(1)} fusion(f32[2560]{0:T(1024)S(1)} %get-tuple-element.491, f32[640]{0:T(1024)S(1)} %get-tuple-element.492, f32[2560]{0:T(1024)S(1)} %get-tuple-element.493, f32[640]{0:T(1024)S(1)} %get-tuple-element.494, f32[2560]{0:T(1024)S(1)} %get-tuple-element.495, f32[640]{0:T(1024)S(1)} %get-tuple-element.496, ...), kind=kOutput, calls=%fused_computation.84.clone.1 | convolution fusion | flops 77008640 | bytes 108037 | tf_op jit(solution)/shard_map/while/body/eval_jaxpr/dot_general | solution.py:89
  254.1 5.8 %fusion.169 = f32[3,640]{1,0:T(4,128)S(1)} fusion(f32[2560]{0:T(1024)S(1)} %get-tuple-element.491, f32[640]{0:T(1024)S(1)} %get-tuple-element.492, f32[2560]{0:T(1024)S(1)} %get-tuple-element.493, f32[640]{0:T(1024)S(1)} %get-tuple-element.494, f32[2560]{0:T(1024)S(1)} %get-tuple-element.495, f32[640]{0:T(1024)S(1)} %get-tuple-element.496, ...), kind=kOutput, calls=%fused_computation.84.clone.1 | convolution fusion | flops 77008640 | bytes 108037 | tf_op jit(solution)/shard_map/while/body/eval_jaxpr/dot_general | solution.py:89
  260.0 5.8 %fusion.169 = f32[3,640]{1,0:T(4,128)S(1)} fusion(f32[2560]{0:T(1024)S(1)} %get-tuple-element.491, f32[640]{0:T(1024)S(1)} %get-tuple-element.492, f32[2560]{0:T(1024)S(1)} %get-tuple-element.493, f32[640]{0:T(1024)S(1)} %get-tuple-element.494, f32[2560]{0:T(1024)S(1)} %get-tuple-element.495, f32[640]{0:T(1024)S(1)} %get-tuple-element.496, ...), kind=kOutput, calls=%fused_computation.84.clone.1 | convolution fusion | flops 77008640 | bytes 108037 | tf_op jit(solution)/shard_map/while/body/eval_jaxpr/dot_general | solution.py:89
  265.9 5.8 %fusion.169 = f32[3,640]{1,0:T(4,128)S(1)} fusion(f32[2560]{0:T(1024)S(1)} %get-tuple-element.491, f32[640]{0:T(1024)S(1)} %get-tuple-element.492, f32[2560]{0:T(1024)S(1)} %get-tuple-element.493, f32[640]{0:T(1024)S(1)} %get-tuple-element.494, f32[2560]{0:T(1024)S(1)} %get-tuple-element.495, f32[640]{0:T(1024)S(1)} %get-tuple-element.496, ...), kind=kOutput, calls=%fused_computation.84.clone.1 | convolution fusion | flops 77008640 | bytes 108037 | tf_op jit(solution)/shard_map/while/body/eval_jaxpr/dot_general | solution.py:89
  271.9 5.8 %fusion.169 = f32[3,640]{1,0:T(4,128)S(1)} fusion(f32[2560]{0:T(1024)S(1)} %get-tuple-element.491, f32[640]{0:T(1024)S(1)} %get-tuple-element.492, f32[2560]{0:T(1024)S(1)} %get-tuple-element.493, f32[640]{0:T(1024)S(1)} %get-tuple-element.494, f32[2560]{0:T(1024)S(1)} %get-tuple-element.495, f32[640]{0:T(1024)S(1)} %get-tuple-element.496, ...), kind=kOutput, calls=%fused_computation.84.clone.1 | convolution fusion | flops 77008640 | bytes 108037 | tf_op jit(solution)/shard_map/while/body/eval_jaxpr/dot_general | solution.py:89
  278.1 40.6 %all-reduce = (f32[3]{0:T(128)S(1)}, f32[3,4]{1,0:T(4,128)S(1)}, f32[3,3]{0,1:T(4,128)S(1)}) all-reduce(f32[3]{0:T(128)S(1)} %get-tuple-element.225, f32[3,4]{1,0:T(4,128)S(1)} %fusion.134, f32[3,3]{0,1:T(4,128)S(1)} %pad_maximum_fusion.4), channel_id=1, replica_groups=mesh['blk'=8,'grp'=4] {'blk','grp'}, use_global_device_ids=true, to_apply=%region_33.34 | all-reduce | flops 24 | bytes 192 | tf_op jit(solution)/shard_map/psum | solution.py:133
  319.1 5.6 %all_gather.15 = f32[6,2560]{1,0:T(8,128)S(1)} all-gather(f32[6,640]{1,0:T(8,128)S(1)} %pad_maximum_fusion), channel_id=1, replica_groups=mesh['blk'=8,'grp'=4] {'grp'}, dimensions={1}, use_global_device_ids=true | all-gather | bytes 76800 | tf_op jit(solution)/shard_map/all_gather | solution.py:70
  347.1 43.3 %while.47 = (s32[]{:T(128)}, f32[3,512]{1,0:T(4,128)S(1)}, f32[7,3,2560]{2,1,0:T(4,128)S(1)}, s32[7]{0:T(128)S(1)}, s32[512]{0:T(512)S(1)}, /*index=5*/f32[3,512...) while((s32[]{:T(128)}, f32[3,512]{1,0:T(4,128)S(1)}, ...), condition=%wide.region_36.37_spmd.clone, body=%wide.region_35.36_spmd.clone.sunk | while | flops 62919172 | bytes 175279 | solution.py:94
  348.5 4.8 %fusion.173 = f32[3,512]{1,0:T(4,128)S(1)} fusion(f32[2560]{0:T(1024)S(1)} %get-tuple-element.504, f32[512]{0:T(512)S(1)} %bitcast.203, f32[2560]{0:T(1024)S(1)} %get-tuple-element.506, f32[512]{0:T(512)S(1)} %bitcast.204, f32[2560]{0:T(1024)S(1)} %get-tuple-element.508, f32[512]{0:T(512)S(1)} %bitcast.202, ...), kind=kOutput, calls=%fused_computation.119.clone.1 | convolution fusion | flops 62917632 | bytes 98821 | tf_op jit(solution)/shard_map/while/body/eval_jaxpr/dot_general | solution.py:89
  354.7 4.8 %fusion.173 = f32[3,512]{1,0:T(4,128)S(1)} fusion(f32[2560]{0:T(1024)S(1)} %get-tuple-element.504, f32[512]{0:T(512)S(1)} %bitcast.203, f32[2560]{0:T(1024)S(1)} %get-tuple-element.506, f32[512]{0:T(512)S(1)} %bitcast.204, f32[2560]{0:T(1024)S(1)} %get-tuple-element.508, f32[512]{0:T(512)S(1)} %bitcast.202, ...), kind=kOutput, calls=%fused_computation.119.clone.1 | convolution fusion | flops 62917632 | bytes 98821 | tf_op jit(solution)/shard_map/while/body/eval_jaxpr/dot_general | solution.py:89
  360.9 4.8 %fusion.173 = f32[3,512]{1,0:T(4,128)S(1)} fusion(f32[2560]{0:T(1024)S(1)} %get-tuple-element.504, f32[512]{0:T(512)S(1)} %bitcast.203, f32[2560]{0:T(1024)S(1)} %get-tuple-element.506, f32[512]{0:T(512)S(1)} %bitcast.204, f32[2560]{0:T(1024)S(1)} %get-tuple-element.508, f32[512]{0:T(512)S(1)} %bitcast.202, ...), kind=kOutput, calls=%fused_computation.119.clone.1 | convolution fusion | flops 62917632 | bytes 98821 | tf_op jit(solution)/shard_map/while/body/eval_jaxpr/dot_general | solution.py:89
  367.0 4.8 %fusion.173 = f32[3,512]{1,0:T(4,128)S(1)} fusion(f32[2560]{0:T(1024)S(1)} %get-tuple-element.504, f32[512]{0:T(512)S(1)} %bitcast.203, f32[2560]{0:T(1024)S(1)} %get-tuple-element.506, f32[512]{0:T(512)S(1)} %bitcast.204, f32[2560]{0:T(1024)S(1)} %get-tuple-element.508, f32[512]{0:T(512)S(1)} %bitcast.202, ...), kind=kOutput, calls=%fused_computation.119.clone.1 | convolution fusion | flops 62917632 | bytes 98821 | tf_op jit(solution)/shard_map/while/body/eval_jaxpr/dot_general | solution.py:89
  379.4 4.8 %fusion.173 = f32[3,512]{1,0:T(4,128)S(1)} fusion(f32[2560]{0:T(1024)S(1)} %get-tuple-element.504, f32[512]{0:T(512)S(1)} %bitcast.203, f32[2560]{0:T(1024)S(1)} %get-tuple-element.506, f32[512]{0:T(512)S(1)} %bitcast.204, f32[2560]{0:T(1024)S(1)} %get-tuple-element.508, f32[512]{0:T(512)S(1)} %bitcast.202, ...), kind=kOutput, calls=%fused_computation.119.clone.1 | convolution fusion | flops 62917632 | bytes 98821 | tf_op jit(solution)/shard_map/while/body/eval_jaxpr/dot_general | solution.py:89
  (170 shorter events, 92.8 us)
Async XLA Ops:
  50.5 12.6 %collective-permute-start = (f32[6,2560]{1,0:T(8,128)S(1)}, f32[6,2560]{1,0:T(8,128)S(1)}, u32[]{:S(2)}, u32[]{:S(2)}) collective-permute-start(f32[6,2560]{1,0:T(8,128)S(1)} %all_gather.12), channel_id=1, source_target_pairs={{0,8},{4,12},{8,16},{12,20},{16,24},{20,28},{1,9},{5,13},{9,17},{1... | collective-permute-start | bytes 184328 | tf_op jit(solution)/shard_map/ppermute | solution.py:20
  53.9 9.2 %collective-permute-start.1 = (f32[6,2560]{1,0:T(8,128)S(1)}, f32[6,2560]{1,0:T(8,128)S(1)}, u32[]{:S(2)}, u32[]{:S(2)}) collective-permute-start(f32[6,2560]{1,0:T(8,128)S(1)} %all_gather.12), channel_id=1, source_target_pairs={{0,4},{4,8},{8,12},{12,16},{16,20},{20,24},{24,28},{1,5},{5,9},{9,... | collective-permute-start | bytes 184328 | tf_op jit(solution)/shard_map/ppermute | solution.py:20
  57.8 6.3 %collective-permute-start.2 = (f32[6,2560]{1,0:T(8,128)S(1)}, f32[6,2560]{1,0:T(8,128)S(1)}, u32[]{:S(2)}, u32[]{:S(2)}) collective-permute-start(f32[6,2560]{1,0:T(8,128)S(1)} %all_gather.12), channel_id=1, source_target_pairs={{4,0},{8,4},{12,8},{16,12},{20,16},{24,20},{28,24},{5,1},{9,5},{13... | collective-permute-start | bytes 184328 | tf_op jit(solution)/shard_map/ppermute | solution.py:20
  59.1 7.2 %collective-permute-start.3 = (f32[6,2560]{1,0:T(8,128)S(1)}, f32[6,2560]{1,0:T(8,128)S(1)}, u32[]{:S(2)}, u32[]{:S(2)}) collective-permute-start(f32[6,2560]{1,0:T(8,128)S(1)} %all_gather.12), channel_id=1, source_target_pairs={{8,0},{12,4},{16,8},{20,12},{24,16},{28,20},{9,1},{13,5},{17,9},{2... | collective-permute-start | bytes 184328 | tf_op jit(solution)/shard_map/ppermute | solution.py:20
  63.1 3.3 copy-start
  66.5 70.2 %copy-start.1 = (f32[3,640]{1,0:T(4,128)S(1)}, f32[3,640]{1,0:T(4,128)}, u32[]{:S(2)}) copy-start(f32[3,640]{1,0:T(4,128)} %param.13) | copy-start | bytes 23044
  142.3 9.2 %collective-permute-start.4 = (f32[6,2560]{1,0:T(8,128)S(1)}, f32[6,2560]{1,0:T(8,128)S(1)}, u32[]{:S(2)}, u32[]{:S(2)}) collective-permute-start(f32[6,2560]{1,0:T(8,128)S(1)} %all_gather.13), channel_id=1, source_target_pairs={{0,8},{4,12},{8,16},{12,20},{16,24},{20,28},{1,9},{5,13},{9,17},{1... | collective-permute-start | bytes 184328 | tf_op jit(solution)/shard_map/ppermute | solution.py:20
  144.6 7.0 %collective-permute-start.5 = (f32[6,2560]{1,0:T(8,128)S(1)}, f32[6,2560]{1,0:T(8,128)S(1)}, u32[]{:S(2)}, u32[]{:S(2)}) collective-permute-start(f32[6,2560]{1,0:T(8,128)S(1)} %all_gather.13), channel_id=1, source_target_pairs={{0,4},{4,8},{8,12},{12,16},{16,20},{20,24},{24,28},{1,5},{5,9},{9,... | collective-permute-start | bytes 184328 | tf_op jit(solution)/shard_map/ppermute | solution.py:20
  148.6 6.3 %collective-permute-start.6 = (f32[6,2560]{1,0:T(8,128)S(1)}, f32[6,2560]{1,0:T(8,128)S(1)}, u32[]{:S(2)}, u32[]{:S(2)}) collective-permute-start(f32[6,2560]{1,0:T(8,128)S(1)} %all_gather.13), channel_id=1, source_target_pairs={{4,0},{8,4},{12,8},{16,12},{20,16},{24,20},{28,24},{5,1},{9,5},{13... | collective-permute-start | bytes 184328 | tf_op jit(solution)/shard_map/ppermute | solution.py:20
  149.9 6.7 %collective-permute-start.7 = (f32[6,2560]{1,0:T(8,128)S(1)}, f32[6,2560]{1,0:T(8,128)S(1)}, u32[]{:S(2)}, u32[]{:S(2)}) collective-permute-start(f32[6,2560]{1,0:T(8,128)S(1)} %all_gather.13), channel_id=1, source_target_pairs={{8,0},{12,4},{16,8},{20,12},{24,16},{28,20},{9,1},{13,5},{17,9},{2... | collective-permute-start | bytes 184328 | tf_op jit(solution)/shard_map/ppermute | solution.py:20
  233.6 9.4 %collective-permute-start.8 = (f32[6,2560]{1,0:T(8,128)S(1)}, f32[6,2560]{1,0:T(8,128)S(1)}, u32[]{:S(2)}, u32[]{:S(2)}) collective-permute-start(f32[6,2560]{1,0:T(8,128)S(1)} %all_gather.14), channel_id=1, source_target_pairs={{0,8},{4,12},{8,16},{12,20},{16,24},{20,28},{1,9},{5,13},{9,17},{1... | collective-permute-start | bytes 184328 | tf_op jit(solution)/shard_map/ppermute | solution.py:20
  235.9 7.1 %collective-permute-start.9 = (f32[6,2560]{1,0:T(8,128)S(1)}, f32[6,2560]{1,0:T(8,128)S(1)}, u32[]{:S(2)}, u32[]{:S(2)}) collective-permute-start(f32[6,2560]{1,0:T(8,128)S(1)} %all_gather.14), channel_id=1, source_target_pairs={{0,4},{4,8},{8,12},{12,16},{16,20},{20,24},{24,28},{1,5},{5,9},{9,... | collective-permute-start | bytes 184328 | tf_op jit(solution)/shard_map/ppermute | solution.py:20
  239.9 6.3 %collective-permute-start.10 = (f32[6,2560]{1,0:T(8,128)S(1)}, f32[6,2560]{1,0:T(8,128)S(1)}, u32[]{:S(2)}, u32[]{:S(2)}) collective-permute-start(f32[6,2560]{1,0:T(8,128)S(1)} %all_gather.14), channel_id=1, source_target_pairs={{4,0},{8,4},{12,8},{16,12},{20,16},{24,20},{28,24},{5,1},{9,5},{13... | collective-permute-start | bytes 184328 | tf_op jit(solution)/shard_map/ppermute | solution.py:20
  241.2 6.7 %collective-permute-start.11 = (f32[6,2560]{1,0:T(8,128)S(1)}, f32[6,2560]{1,0:T(8,128)S(1)}, u32[]{:S(2)}, u32[]{:S(2)}) collective-permute-start(f32[6,2560]{1,0:T(8,128)S(1)} %all_gather.14), channel_id=1, source_target_pairs={{8,0},{12,4},{16,8},{20,12},{24,16},{28,20},{9,1},{13,5},{17,9},{2... | collective-permute-start | bytes 184328 | tf_op jit(solution)/shard_map/ppermute | solution.py:20
  319.0 27.4 %copy-start.4 = (f32[3,640]{1,0:T(4,128)}, f32[3,640]{1,0:T(4,128)S(1)}, u32[]{:S(2)}) copy-start(f32[3,640]{1,0:T(4,128)S(1)} %multiply_add_fusion) | copy-start | bytes 23044
  324.6 12.7 %collective-permute-start.12 = (f32[6,2560]{1,0:T(8,128)S(1)}, f32[6,2560]{1,0:T(8,128)S(1)}, u32[]{:S(2)}, u32[]{:S(2)}) collective-permute-start(f32[6,2560]{1,0:T(8,128)S(1)} %all_gather.15), channel_id=1, source_target_pairs={{0,12},{4,16},{8,20},{12,24},{16,28},{1,13},{5,17},{9,21},{13,25},... | collective-permute-start | bytes 184328 | tf_op jit(solution)/shard_map/ppermute | solution.py:20
  328.1 10.8 %collective-permute-start.13 = (f32[6,2560]{1,0:T(8,128)S(1)}, f32[6,2560]{1,0:T(8,128)S(1)}, u32[]{:S(2)}, u32[]{:S(2)}) collective-permute-start(f32[6,2560]{1,0:T(8,128)S(1)} %all_gather.15), channel_id=1, source_target_pairs={{0,8},{4,12},{8,16},{12,20},{16,24},{20,28},{1,9},{5,13},{9,17},{1... | collective-permute-start | bytes 184328 | tf_op jit(solution)/shard_map/ppermute | solution.py:20
  331.2 7.8 %collective-permute-start.14 = (f32[6,2560]{1,0:T(8,128)S(1)}, f32[6,2560]{1,0:T(8,128)S(1)}, u32[]{:S(2)}, u32[]{:S(2)}) collective-permute-start(f32[6,2560]{1,0:T(8,128)S(1)} %all_gather.15), channel_id=1, source_target_pairs={{0,4},{4,8},{8,12},{12,16},{16,20},{20,24},{24,28},{1,5},{5,9},{9,... | collective-permute-start | bytes 184328 | tf_op jit(solution)/shard_map/ppermute | solution.py:20
  334.7 6.3 %collective-permute-start.15 = (f32[6,2560]{1,0:T(8,128)S(1)}, f32[6,2560]{1,0:T(8,128)S(1)}, u32[]{:S(2)}, u32[]{:S(2)}) collective-permute-start(f32[6,2560]{1,0:T(8,128)S(1)} %all_gather.15), channel_id=1, source_target_pairs={{4,0},{8,4},{12,8},{16,12},{20,16},{24,20},{28,24},{5,1},{9,5},{13... | collective-permute-start | bytes 184328 | tf_op jit(solution)/shard_map/ppermute | solution.py:20
  336.0 8.4 %collective-permute-start.16 = (f32[6,2560]{1,0:T(8,128)S(1)}, f32[6,2560]{1,0:T(8,128)S(1)}, u32[]{:S(2)}, u32[]{:S(2)}) collective-permute-start(f32[6,2560]{1,0:T(8,128)S(1)} %all_gather.15), channel_id=1, source_target_pairs={{8,0},{12,4},{16,8},{20,12},{24,16},{28,20},{9,1},{13,5},{17,9},{2... | collective-permute-start | bytes 184328 | tf_op jit(solution)/shard_map/ppermute | solution.py:20
  337.3 53.1 %copy-start.5 = (f32[3,4]{1,0:T(4,128)}, f32[3,4]{1,0:T(4,128)S(1)}, u32[]{:S(2)}) copy-start(f32[3,4]{1,0:T(4,128)S(1)} %multiply_add_fusion.7) | copy-start | bytes 148
  337.4 9.0 %collective-permute-start.17 = (f32[6,2560]{1,0:T(8,128)S(1)}, f32[6,2560]{1,0:T(8,128)S(1)}, u32[]{:S(2)}, u32[]{:S(2)}) collective-permute-start(f32[6,2560]{1,0:T(8,128)S(1)} %all_gather.15), channel_id=1, source_target_pairs={{12,0},{16,4},{20,8},{24,12},{28,16},{13,1},{17,5},{21,9},{25,13},... | collective-permute-start | bytes 184328 | tf_op jit(solution)/shard_map/ppermute | solution.py:20
  346.4 0.7 copy-start.2
  346.4 0.7 copy-start.3
where the time goes:
time: 395 us; the launch traced here: 391 us
  blocking collectives  186 us (47%)
  matrix products  124 us (31%)
  starting transfers between devices  42.1 us (11%)
  waiting for transfers between devices  20.3 us (5%)
  other arithmetic  9.73 us (2%)
  local copies, waits for them, and re-layouts  7.71 us (2%)
    psum x3, blocking collectives, shards(): lax.psum((local_dots, jnp.sum(image_head * image_head, axis=1), jnp.dot(i...  122 us
    dot_general x22, matrix products, add_slab(): jnp.dot(values, tile, precision=precise, preferred_element_type=jnp.float32)  121 us
    ppermute x18, starting transfers between devices, from_behind(): lax.ppermute(value, axis, [(source, source + steps) for source in range(i...  42.1 us
    psum x1, blocking collectives, shards(): lax.psum((jnp.sum(source_values * source_values, axis=1), jnp.dot(source_...  42 us
    all_gather x4, blocking collectives, near_slabs(): slab = lax.all_gather(block, 'grp', axis=1, tiled=True)  22.2 us
    ppermute x18, waiting for transfers between devices, from_behind(): lax.ppermute(value, axis, [(source, source + steps) for source in range(i...  20.3 us
  transfers between devices with their start and end apart: 18, of which 9 were waited for; matrix products, arithmetic and copies ran while one was open for 1% of the time, Pallas kernels for 0%

commit v1 on v0

v1 whole, which is shorter than its diff:
```python
import functools
import math

import jax
import jax.numpy as jnp
from jax import lax
from jax.experimental import pallas as pl
from jax.experimental.pallas import tpu as pltpu
from jax.sharding import PartitionSpec as P

ITERS = 3
REACH = 2
C = 3
thin_factor = 0.6
tiny = 1e-06
LANES = 128
GROUP = 64
MESH = pl.DeviceIdType.MESH


def least_squares(hessenberg, beta):
    count = len(hessenberg)
    right_side = [beta] + [jnp.zeros_like(beta) for k in range(count)]
    upper, cosines, sines = [], [], []
    for k in range(count):
        column = list(hessenberg[k])
        for i in range(k):
            top = cosines[i] * column[i] + sines[i] * column[i + 1]
            lower = -sines[i] * column[i] + cosines[i] * column[i + 1]
            column[i] = top
            column[i + 1] = lower
        radius = jnp.sqrt(column[k] * column[k] + column[k + 1] * column[k + 1])
        cosine = column[k] / radius
        sine = column[k + 1] / radius
        column[k] = radius
        cosines.append(cosine)
        sines.append(sine)
        right_side[k + 1] = -sine * right_side[k]
        right_side[k] = cosine * right_side[k]
        upper.append(column[: k + 1])
    solved = [None] * count
    for k in reversed(range(count)):
        running = right_side[k]
        for j in range(k + 1, count):
            running = running - upper[j][k] * solved[j]
        solved[k] = running / upper[k][k]
    return solved


def kernel(
    n_blk, n_grp, sub, tsub, scale_x, scale_y, root_n,
    own_ref, tgt_ref, out_w, out_m, out_p,
    kbuf, rowb, accb, recv0, recv1, recv2, recv3, send0, send1, send2, send3,
    ccols, v0, v1, v2, wn, send_sem, recv_sem,
):
    blk = lax.axis_index("blk")
    grp = lax.axis_index("grp")
    peers = n_blk * n_grp
    wide = REACH + 1
    near = (2 * wide + 1) * n_grp
    recvs = (recv0, recv1, recv2, recv3)
    sends = (send0, send1, send2, send3)
    heads = (v0, v1, v2)
    own_near = wide * n_grp

    def target(p):
        e = p // n_grp
        h = p % n_grp
        return lax.rem(blk + e, n_blk), lax.rem(grp + h, n_grp), e

    barrier = pltpu.get_barrier_semaphore()

    def greet(p, carry):
        tb, tg, e = target(p)
        pl.semaphore_signal(barrier, inc=1, device_id=(tb, tg), device_id_type=MESH)
        return carry

    lax.fori_loop(1, peers, greet, 0)

    lane = lax.broadcasted_iota(jnp.int32, (1, LANES), 1)
    sub8 = lax.broadcasted_iota(jnp.int32, (8, LANES), 0)
    sub16 = lax.broadcasted_iota(jnp.int32, (16, LANES), 0)

    def rows16(f):
        return jnp.where(sub16 < sub, f[0:1], jnp.where(sub16 < 2 * sub, f[1:2], f[2:3]))

    x_own = own_ref[0:sub]
    y_own = own_ref[sub : 2 * sub]
    z_own = own_ref[2 * sub : 3 * sub]

    def basis_rows(x, y, z):
        return (
            jnp.full_like(x, 1.0 / root_n),
            (x * (2.0 / (n_blk * scale_x)) - 1.0) * (1.0 / root_n),
            y * (2.0 / (scale_y * root_n)),
            z * (2.0 / (scale_y * root_n)),
        )

    p_own = basis_rows(x_own, y_own, z_own)

    def total(a):
        return jnp.sum(jnp.sum(a, axis=0, keepdims=True), axis=1, keepdims=True)

    def dots_row(w, others):
        row = jnp.zeros((1, LANES), jnp.float32)
        for c in range(C):
            wc = w[c * sub : (c + 1) * sub]
            terms = [(i, total(wc * o[c * sub : (c + 1) * sub])) for i, o in enumerate(others)]
            terms.append((3, total(wc * wc)))
            terms += [(4 + j, total(wc * p_own[j])) for j in range(4)]
            for q, value in terms:
                row = jnp.where(lane == 16 * c + q, value, row)
        return row

    vals = own_ref[16:32]
    row0 = dots_row(vals, [])
    send0[0:16] = own_ref[0:16]
    send0[16:31] = own_ref[16:31]
    send0[31:32] = row0
    pl.semaphore_wait(barrier, peers - 1)

    def copy_to(r, p):
        tb, tg, e = target(p)
        return pltpu.make_async_remote_copy(
            src_ref=sends[r],
            dst_ref=recvs[r].at[p],
            send_sem=send_sem.at[r],
            recv_sem=recv_sem.at[r],
            device_id=(tb, tg),
            device_id_type=MESH,
        )

    def start_round(r):
        def body(p, carry):
            copy_to(r, p).start()
            return carry

        lax.fori_loop(1, peers, body, 0)
        recvs[r][0] = sends[r][...]

    def wait_round(r):
        landed = recvs[r].at[pl.ds(1, peers - 1)]
        pltpu.make_async_copy(landed, landed, recv_sem.at[r]).wait()
        last = recvs[r].shape[1] - 1
        row = jnp.sum(recvs[r][:, last, :], axis=0, keepdims=True)
        b = jnp.broadcast_to(row, (8, LANES))
        t = jnp.where(
            sub8 == 0, b, jnp.where(sub8 == 1, pltpu.roll(b, LANES - 16, 1), pltpu.roll(b, LANES - 32, 1))
        )
        return [jnp.broadcast_to(t[:, q : q + 1], (8, LANES)) for q in range(8)]

    send3[...] = jnp.zeros((8, LANES), jnp.float32)
    start_round(0)

    for c in range(C):
        for s in range(sub):
            line = jnp.broadcast_to(own_ref[c * sub + s : c * sub + s + 1, :], (LANES, LANES))
            rowb[c, s * LANES : (s + 1) * LANES, :] = line.T

    sums = wait_round(0)
    beta = jnp.sqrt(sums[3] + tiny)
    inv_beta = 1.0 / beta
    tails = [[jnp.zeros((8, LANES), jnp.float32)] * 4]
    moments = [[sums[4 + j] * inv_beta for j in range(4)]]
    scale0 = rows16(inv_beta)

    def slot_of(j):
        d = j // n_grp - wide
        place = blk + d
        valid = jnp.logical_and(place >= 0, place < n_blk)
        return lax.rem(n_blk - d, n_blk) * n_grp + j % n_grp, valid

    def fill(j, carry):
        slot, valid = slot_of(j)
        keep = jnp.where(valid, 1.0, 0.0).astype(jnp.float32)
        ccols[j] = recv0[slot, 0:16]
        v0[j] = recv0[slot, 16:32] * (scale0 * keep)
        return carry

    lax.fori_loop(0, near, fill, 0)

    ones8 = jnp.ones((8, LANES), jnp.float32)

    def lane_sums(c, s):
        tile = accb[c, s * LANES : (s + 1) * LANES, :]
        return lax.dot_general(
            ones8, tile, (((1,), (1,)), ((), ())),
            precision=lax.Precision.HIGHEST, preferred_element_type=jnp.float32,
        )[0:1]

    inner = (2 * REACH + 1) * n_grp

    def apply(values, first):
        def group(rg, carry):
            at = pl.ds(pl.multiple_of(rg * GROUP, GROUP), GROUP)
            if first:
                rx, ry, rz = rowb[0, at, :], rowb[1, at, :], rowb[2, at, :]

            def step(j, acc):
                acc = list(acc)
                jn = j + n_grp
                for s in range(sub):
                    if first:
                        dx = rx - ccols[jn, s : s + 1, :]
                        dy = ry - ccols[jn, sub + s : sub + s + 1, :]
                        dz = rz - ccols[jn, 2 * sub + s : 2 * sub + s + 1, :]
                        tile = jnp.exp2(-(dx * dx + dy * dy + dz * dz))
                        kbuf[j * sub + s, at, :] = tile
                    else:
                        tile = kbuf[j * sub + s, at, :]
                    for c in range(C):
                        acc[c] = acc[c] + tile * values[jn, c * sub + s : c * sub + s + 1, :]
                return tuple(acc)

            zero = jnp.zeros((GROUP, LANES), jnp.float32)
            acc = lax.fori_loop(0, inner, step, (zero,) * C)
            for c in range(C):
                accb[c, at, :] = acc[c]
            return carry

        lax.fori_loop(0, sub * LANES // GROUP, group, 0)

    hessenberg = []
    for k in range(ITERS):
        apply(heads[k], k == 0)
        image_tail = moments[k]
        block = sends[k + 1] if k + 1 < ITERS else wn.at[0]
        for c in range(C):
            for s in range(sub):
                line = lane_sums(c, s)
                if k > 0:
                    for j in range(4):
                        line = line + tails[k][j][c : c + 1] * p_own[j][s : s + 1]
                block[c * sub + s : c * sub + s + 1, :] = line
        row = dots_row(block[...], [heads[i][own_near] for i in range(k + 1)])
        last = sends[k + 1].shape[0] - 1
        sends[k + 1][last : last + 1, :] = row
        start_round(k + 1)
        if k + 1 == ITERS:
            for c in range(4):
                for s in range(tsub):
                    line = jnp.broadcast_to(tgt_ref[c * tsub + s : c * tsub + s + 1, :], (LANES, LANES))
                    rowb[c, s * LANES : (s + 1) * LANES, :] = line.T
        sums = wait_round(k + 1)
        full_sq = sums[3]
        for j in range(4):
            full_sq = full_sq + image_tail[j] * image_tail[j]
        rest_tail = list(image_tail)
        rest_moment = [sums[4 + j] for j in range(4)]
        column = []
        for i in range(k + 1):
            factor = sums[i]
            for j in range(4):
                factor = factor + tails[i][j] * image_tail[j]
            full_sq = full_sq - factor * factor
            for j in range(4):
                rest_tail[j] = rest_tail[j] - factor * tails[i][j]
                rest_moment[j] = rest_moment[j] - factor * moments[i][j]
            column.append(factor)
        length = jnp.sqrt(full_sq + tiny)
        inv_length = 1.0 / length
        hessenberg.append(column + [length])
        if k + 1 < ITERS:
            tails.append([t * inv_length for t in rest_tail])
            moments.append([m * inv_length for m in rest_moment])
            scale = rows16(inv_length)
            factors = [rows16(f * inv_length) for f in column]

            def advance(j, carry, k=k, scale=scale, factors=factors):
                slot, valid = slot_of(j)
                keep = jnp.where(valid, 1.0, 0.0).astype(jnp.float32)
                v = recvs[k + 1][slot] * (scale * keep)
                for i in range(k + 1):
                    v = v - factors[i] * heads[i][j]
                heads[k + 1][j] = v
                return carry

            lax.fori_loop(0, near, advance, 0)

    solved = least_squares(hessenberg, beta)
    poly = []
    for j in range(4):
        p = solved[0] * tails[0][j]
        for k in range(1, ITERS):
            p = p + solved[k] * tails[k][j]
        poly.append(p)
    lane8 = lax.broadcasted_iota(jnp.int32, (8, LANES), 1)
    packed = poly[3]
    for j in range(3):
        packed = jnp.where(lane8 == j, poly[j], packed)
    out_p[...] = packed
    spread = [rows16(y) for y in solved]

    def combine(j, carry):
        wn[j] = spread[0] * v0[j] + spread[1] * v1[j] + spread[2] * v2[j]
        return carry

    lax.fori_loop(0, near, combine, 0)
    out_w[...] = wn[own_near]

    def tgroup(rg, carry):
        at = pl.ds(pl.multiple_of(rg * GROUP, GROUP), GROUP)
        rx, ry, rz, own = rowb[0, at, :], rowb[1, at, :], rowb[2, at, :], rowb[3, at, :]
        zero = jnp.zeros((GROUP, LANES), jnp.float32)
        for c in range(C):
            accb[c, at, :] = zero

        def slab(d, carry2):
            def step(g, acc):
                acc = list(acc)
                jn = d * n_grp + g
                for s in range(sub):
                    dx = rx - ccols[jn, s : s + 1, :]
                    dy = ry - ccols[jn, sub + s : sub + s + 1, :]
                    dz = rz - ccols[jn, 2 * sub + s : 2 * sub + s + 1, :]
                    tile = jnp.exp2(-(dx * dx + dy * dy + dz * dz))
                    for c in range(C):
                        acc[c] = acc[c] + tile * wn[jn, c * sub + s : c * sub + s + 1, :]
                return tuple(acc)

            acc = lax.fori_loop(0, n_grp, step, (zero,) * C)
            away = (d - wide).astype(jnp.float32)
            hit = jnp.abs(own - away) <= REACH + 0.5
            for c in range(C):
                accb[c, at, :] = accb[c, at, :] + jnp.where(hit, acc[c], 0.0)
            return carry2

        lax.fori_loop(0, 2 * wide + 1, slab, 0)
        return carry

    lax.fori_loop(0, tsub * LANES // GROUP, tgroup, 0)
    for r in range(ITERS + 1):
        sent = recvs[r].at[pl.ds(1, peers - 1)]
        pltpu.make_async_copy(sent, sent, send_sem.at[r]).wait()
    q_own = basis_rows(tgt_ref[0:tsub], tgt_ref[tsub : 2 * tsub], tgt_ref[2 * tsub : 3 * tsub])
    out_m[...] = jnp.zeros((16, LANES), jnp.float32)
    for c in range(C):
        for s in range(tsub):
            line = lane_sums(c, s)
            for j in range(4):
                line = line + poly[j][c : c + 1] * q_own[j][s : s + 1]
            out_m[c * tsub + s : c * tsub + s + 1, :] = line


def shards(source_coords, source_values, target_coords, target_owner):
    own_rows = source_coords.shape[1]
    own_tgt = target_coords.shape[1]
    n_grp = lax.axis_size("grp")
    n_blk = lax.axis_size("blk")
    sub = own_rows // LANES
    tsub = own_tgt // LANES
    slab_len = own_rows * n_grp
    root_n = math.sqrt(slab_len * n_blk)
    log2e = 1.0 / math.log(2.0)
    scale_x = math.sqrt(thin_factor * log2e)
    scale_y = math.sqrt(4.0 * slab_len * log2e)
    blk = lax.axis_index("blk")
    scales = jnp.array([[scale_x], [scale_y], [scale_y]], jnp.float32)
    shift = jnp.array([[0.0], [0.5], [0.5]], jnp.float32)
    pad = jnp.zeros((1, LANES), jnp.float32)
    own = jnp.concatenate(
        [
            ((source_coords - shift) * scales).reshape(3 * sub, LANES),
            pad,
            source_values.reshape(3 * sub, LANES),
            pad,
        ]
    )
    tgt = jnp.concatenate(
        [
            ((target_coords - shift) * scales).reshape(3 * tsub, LANES),
            (target_owner - blk).astype(jnp.float32).reshape(tsub, LANES),
        ]
    )
    peers = n_blk * n_grp
    near = (2 * REACH + 3) * n_grp
    inner = (2 * REACH + 1) * n_grp
    f32 = jnp.float32
    vmem = pl.BlockSpec(memory_space=pltpu.VMEM)
    out_w, out_m, out_p = pl.pallas_call(
        functools.partial(kernel, n_blk, n_grp, sub, tsub, scale_x, scale_y, root_n),
        out_shape=(
            jax.ShapeDtypeStruct((16, LANES), f32),
            jax.ShapeDtypeStruct((16, LANES), f32),
            jax.ShapeDtypeStruct((8, LANES), f32),
        ),
        in_specs=[vmem, vmem],
        out_specs=(vmem, vmem, vmem),
        scratch_shapes=[
            pltpu.VMEM((inner * sub, own_rows, LANES), f32),
            pltpu.VMEM((4, own_rows, LANES), f32),
            pltpu.VMEM((C, own_rows, LANES), f32),
            pltpu.VMEM((peers, 32, LANES), f32),
            pltpu.VMEM((peers, 16, LANES), f32),
            pltpu.VMEM((peers, 16, LANES), f32),
            pltpu.VMEM((peers, 8, LANES), f32),
            pltpu.VMEM((32, LANES), f32),
            pltpu.VMEM((16, LANES), f32),
            pltpu.VMEM((16, LANES), f32),
            pltpu.VMEM((8, LANES), f32),
            pltpu.VMEM((near, 16, LANES), f32),
            pltpu.VMEM((near, 16, LANES), f32),
            pltpu.VMEM((near, 16, LANES), f32),
            pltpu.VMEM((near, 16, LANES), f32),
            pltpu.VMEM((near, 16, LANES), f32),
            pltpu.SemaphoreType.DMA((4,)),
            pltpu.SemaphoreType.DMA((4,)),
        ],
        compiler_params=pltpu.CompilerParams(
            collective_id=0, has_side_effects=True, vmem_limit_bytes=60 * 1024 * 1024
        ),
    )(own, tgt)
    weights = out_w[: C * sub].reshape(C, own_rows)
    mapped = out_m[: C * tsub].reshape(C, own_tgt)
    return weights, out_p[:C, :4], mapped


def solution(mesh):
    return jax.shard_map(
        shards,
        mesh=mesh,
        in_specs=(
            P(None, ("blk", "grp")),
            P(None, ("blk", "grp")),
            P(None, ("blk", "grp")),
            P(("blk", "grp")),
        ),
        out_specs=(P(None, ("blk", "grp")), P(), P(None, ("blk", "grp"))),
        check_vma=False,
    )
```

time: 395 us -> 118 us (0.30)
  blocking collectives: 186 us -> 0 us
  matrix products: 124 us -> 0 us
  Pallas kernels: 0 us -> 111 us
  starting transfers between devices: 42.1 us -> 0 us
  waiting for transfers between devices: 20.3 us -> 0 us
  other arithmetic: 9.73 us -> 2.04 us
  local copies, waits for them, and re-layouts: 7.71 us -> 3.37 us
    psum x4 -> x0, blocking collectives: 164 us -> none  [the longest x3 122 us: shards(): lax.psum((local_dots, jnp.sum(image_head * image_head, axis=1), jnp.dot(i...]
    dot_general x29 -> x0, matrix products: 124 us -> none  [the longest x22 121 us: add_slab(): jnp.dot(values, tile, precision=precise, preferred_element_type=jnp.float32)]
    pallas_call x0 -> x1, Pallas kernels: none -> 111 us  [shards(): pl.pallas_call(functools.partial(kernel, n_blk, n_grp, sub, tsub, scale_x...]
    ppermute x18 -> x0, starting transfers between devices: 42.1 us -> none  [from_behind(): lax.ppermute(value, axis, [(source, source + steps) for source in range(i...]
    all_gather x4 -> x0, blocking collectives: 22.2 us -> none  [near_slabs(): slab = lax.all_gather(block, 'grp', axis=1, tiled=True)]
    ppermute x18 -> x0, waiting for transfers between devices: 20.3 us -> none  [from_behind(): lax.ppermute(value, axis, [(source, source + steps) for source in range(i...]
    le x7 -> x0, other arithmetic: 4.56 us -> none  [add_slab(): tile = jnp.where((jnp.abs(owners - slab) <= reach)[None, :], tile, 0.0)]
    dynamic_slice x7 -> x0, local copies, waits for them, and re-layouts: 4.12 us -> none  [apply_near(): lax.scan(add_slab, start, (near_coords, near_values, labels))]
  transfers between devices with their start and end apart: 18 -> 0, of which waited for: 9 -> 0; matrix products, arithmetic and copies ran while one was open for 1% -> 0% of each run, Pallas kernels for 0% -> 0%
where the time goes in v1:
time: 118 us
  Pallas kernels  111 us (94%)
  local copies, waits for them, and re-layouts  3.37 us (3%)
  other arithmetic  2.04 us (2%)
    pallas_call x1, Pallas kernels, shards(): pl.pallas_call(functools.partial(kernel, n_blk, n_grp, sub, tsub, scale_x...  111 us

profile of v1, /device:TPU:0, one launch (start us, length us, event | category | flops | bytes accessed | tf_op | source)
XLA Modules:
  0.0 117.6 jit_solution(10917031079114094305)
XLA Ops:
  0.6 0.0 copy-start
  0.6 0.7 convert_bitcast_fusion
  1.3 0.0 copy-done
  1.3 0.0 copy-start.2
  1.3 0.0 copy-start.5
  1.3 0.0 copy-start.6
  1.4 0.7 copy-done.2
  2.0 0.0 copy-done.5
  2.0 0.0 copy-done.6
  2.0 0.1 add_multiply_fusion.1
  2.1 0.0 copy-start.1
  2.1 0.6 pad_maximum_fusion.1.tgt_ref
  2.7 0.1 copy-done.1
  2.8 0.1 add_multiply_fusion
  2.9 0.6 pad_maximum_fusion.own_ref
  3.5 111.5 %shard_map.85 = (f32[16,128]{1,0:T(8,128)}, f32[16,128]{1,0:T(8,128)}, f32[8,128]{1,0:T(8,128)}) custom-call(f32[32,128]{1,0:T(8,128)} %pad_maximum_fusion.own_ref, f32[16,128]{1,0:T(8,128)} %pad_maximum_fusion.1.tgt_ref), custom_call_target="tpu_custom_call" | custom-call | tf_op jit(solution)/shard_map/pallas_call | solution.py:380
  115.0 0.0 copy-start.4
  115.0 0.7 copy-done.4
  115.7 0.0 copy-start.7
  115.7 0.0 copy-start.3
  115.7 0.6 reshape.28
  116.3 0.1 copy-done.7
  116.4 0.6 slice.10
  117.0 0.0 copy-done.3
  117.0 0.6 reshape.29
  (4 shorter events, 0.0 us)
Async XLA Ops:
  0.6 0.7 copy-start
  1.3 0.7 copy-start.2
  1.3 0.7 copy-start.5
  1.3 0.7 copy-start.6
  2.1 0.7 copy-start.1
  115.0 0.7 copy-start.4
  115.7 0.7 copy-start.7
  115.7 1.3 %copy-start.3 = (f32[16,128]{1,0:T(8,128)S(1)}, f32[16,128]{1,0:T(8,128)}, u32[]{:S(2)}) copy-start(f32[16,128]{1,0:T(8,128)} %get-tuple-element.8) | copy-start | bytes 24580

commit v2 on v1

--- a/solution.py
+++ b/solution.py
@@ -15,6 +15,7 @@
 tiny = 1e-06
 LANES = 128
 GROUP = 64
+HELD = 3
 MESH = pl.DeviceIdType.MESH
 
 
@@ -50,7 +51,7 @@
 def kernel(
     n_blk, n_grp, sub, tsub, scale_x, scale_y, root_n,
     own_ref, tgt_ref, out_w, out_m, out_p,
-    kbuf, rowb, accb, recv0, recv1, recv2, recv3, send0, send1, send2, send3,
+    kbuf, fbuf, rowb, trowb, accb, recv0, recv1, recv2, recv3, send0, send1, send2, send3,
     ccols, v0, v1, v2, wn, send_sem, recv_sem,
 ):
     blk = lax.axis_index("blk")
@@ -149,13 +150,17 @@
         )
         return [jnp.broadcast_to(t[:, q : q + 1], (8, LANES)) for q in range(8)]
 
-    send3[...] = jnp.zeros((8, LANES), jnp.float32)
     start_round(0)
 
     for c in range(C):
         for s in range(sub):
             line = jnp.broadcast_to(own_ref[c * sub + s : c * sub + s + 1, :], (LANES, LANES))
             rowb[c, s * LANES : (s + 1) * LANES, :] = line.T
+
+    for c in range(4):
+        for s in range(tsub):
+            line = jnp.broadcast_to(tgt_ref[c * tsub + s : c * tsub + s + 1, :], (LANES, LANES))
+            trowb[c, s * LANES : (s + 1) * LANES, :] = line.T
 
     sums = wait_round(0)
     beta = jnp.sqrt(sums[3] + tiny)
@@ -183,10 +188,7 @@
 
     def lane_sums(c, s):
         tile = accb[c, s * LANES : (s + 1) * LANES, :]
-        return lax.dot_general(
-            ones8, tile, (((1,), (1,)), ((), ())),
-            precision=lax.Precision.HIGHEST, preferred_element_type=jnp.float32,
-        )[0:1]
+        return jnp.sum(tile.T, axis=0, keepdims=True)
 
     inner = (2 * REACH + 1) * n_grp
 
@@ -219,6 +221,24 @@
             return carry
 
         lax.fori_loop(0, sub * LANES // GROUP, group, 0)
+
+    def make_tiles(buf, base, low, high):
+        def group(rg, carry):
+            at = pl.ds(pl.multiple_of(rg * GROUP, GROUP), GROUP)
+            rx, ry, rz = trowb[0, at, :], trowb[1, at, :], trowb[2, at, :]
+
+            def step(jn, carry2):
+                for s in range(sub):
+                    dx = rx - ccols[jn, s : s + 1, :]
+                    dy = ry - ccols[jn, sub + s : sub + s + 1, :]
+                    dz = rz - ccols[jn, 2 * sub + s : 2 * sub + s + 1, :]
+                    tile = jnp.exp2(-(dx * dx + dy * dy + dz * dz))
+                    buf[(jn - base * n_grp) * sub + s, at, :] = tile
+                return carry2
+
+            return lax.fori_loop(low * n_grp, high * n_grp, step, carry)
+
+        lax.fori_loop(0, tsub * LANES // GROUP, group, 0)
 
     hessenberg = []
     for k in range(ITERS):
@@ -236,11 +256,12 @@
         last = sends[k + 1].shape[0] - 1
         sends[k + 1][last : last + 1, :] = row
         start_round(k + 1)
-        if k + 1 == ITERS:
-            for c in range(4):
-                for s in range(tsub):
-                    line = jnp.broadcast_to(tgt_ref[c * tsub + s : c * tsub + s + 1, :], (LANES, LANES))
-                    rowb[c, s * LANES : (s + 1) * LANES, :] = line.T
+        if k == 0:
+            make_tiles(fbuf, 0, 0, 2)
+        elif k == 1:
+            make_tiles(fbuf, 0, 2, HELD)
+        elif k + 1 == ITERS:
+            make_tiles(kbuf, HELD, HELD, 2 * wide + 1)
         sums = wait_round(k + 1)
         full_sq = sums[3]
         for j in range(4):
@@ -300,32 +321,33 @@
 
     def tgroup(rg, carry):
         at = pl.ds(pl.multiple_of(rg * GROUP, GROUP), GROUP)
-        rx, ry, rz, own = rowb[0, at, :], rowb[1, at, :], rowb[2, at, :], rowb[3, at, :]
+        own = trowb[3, at, :]
         zero = jnp.zeros((GROUP, LANES), jnp.float32)
         for c in range(C):
             accb[c, at, :] = zero
 
-        def slab(d, carry2):
-            def step(g, acc):
-                acc = list(acc)
-                jn = d * n_grp + g
-                for s in range(sub):
-                    dx = rx - ccols[jn, s : s + 1, :]
-                    dy = ry - ccols[jn, sub + s : sub + s + 1, :]
-                    dz = rz - ccols[jn, 2 * sub + s : 2 * sub + s + 1, :]
-                    tile = jnp.exp2(-(dx * dx + dy * dy + dz * dz))
-                    for c in range(C):
-                        acc[c] = acc[c] + tile * wn[jn, c * sub + s : c * sub + s + 1, :]
-                return tuple(acc)
-
-            acc = lax.fori_loop(0, n_grp, step, (zero,) * C)
-            away = (d - wide).astype(jnp.float32)
-            hit = jnp.abs(own - away) <= REACH + 0.5
-            for c in range(C):
-                accb[c, at, :] = accb[c, at, :] + jnp.where(hit, acc[c], 0.0)
-            return carry2
-
-        lax.fori_loop(0, 2 * wide + 1, slab, 0)
+        def slabs_of(buf, base, low, high):
+            def slab(d, carry2):
+                def step(g, acc):
+                    acc = list(acc)
+                    jn = d * n_grp + g
+                    for s in range(sub):
+                        tile = buf[(jn - base * n_grp) * sub + s, at, :]
+                        for c in range(C):
+                            acc[c] = acc[c] + tile * wn[jn, c * sub + s : c * sub + s + 1, :]
+                    return tuple(acc)
+
+                acc = lax.fori_loop(0, n_grp, step, (zero,) * C)
+                away = (d - wide).astype(jnp.float32)
+                hit = jnp.abs(own - away) <= REACH + 0.5
+                for c in range(C):
+                    accb[c, at, :] = accb[c, at, :] + jnp.where(hit, acc[c], 0.0)
+                return carry2
+
+            lax.fori_loop(low, high, slab, 0)
+
+        slabs_of(fbuf, 0, 0, HELD)
+        slabs_of(kbuf, HELD, HELD, 2 * wide + 1)
         return carry
 
     lax.fori_loop(0, tsub * LANES // GROUP, tgroup, 0)
@@ -388,16 +410,18 @@
         out_specs=(vmem, vmem, vmem),
         scratch_shapes=[
             pltpu.VMEM((inner * sub, own_rows, LANES), f32),
-            pltpu.VMEM((4, own_rows, LANES), f32),
+            pltpu.VMEM((HELD * n_grp * sub, own_tgt, LANES), f32),
+            pltpu.VMEM((3, own_rows, LANES), f32),
+            pltpu.VMEM((4, own_tgt, LANES), f32),
             pltpu.VMEM((C, own_rows, LANES), f32),
             pltpu.VMEM((peers, 32, LANES), f32),
             pltpu.VMEM((peers, 16, LANES), f32),
             pltpu.VMEM((peers, 16, LANES), f32),
-            pltpu.VMEM((peers, 8, LANES), f32),
+            pltpu.VMEM((peers, 1, LANES), f32),
             pltpu.VMEM((32, LANES), f32),
             pltpu.VMEM((16, LANES), f32),
             pltpu.VMEM((16, LANES), f32),
-            pltpu.VMEM((8, LANES), f32),
+            pltpu.VMEM((1, LANES), f32),
             pltpu.VMEM((near, 16, LANES), f32),
             pltpu.VMEM((near, 16, LANES), f32),
             pltpu.VMEM((near, 16, LANES), f32),
@@ -407,7 +431,7 @@
             pltpu.SemaphoreType.DMA((4,)),
         ],
         compiler_params=pltpu.CompilerParams(
-            collective_id=0, has_side_effects=True, vmem_limit_bytes=60 * 1024 * 1024
+            collective_id=0, has_side_effects=True, vmem_limit_bytes=63 * 1024 * 1024
         ),
     )(own, tgt)
     weights = out_w[: C * sub].reshape(C, own_rows)

time: 118 us -> 101 us (0.86)
  Pallas kernels: 111 us -> 93.9 us
    pallas_call x1, Pallas kernels: 111 us -> 93.9 us  [shards(): pl.pallas_call(functools.partial(kernel, n_blk, n_grp, sub, tsub, scale_x...]
where the time goes in v2:
time: 101 us; the launch traced here: 100 us
  Pallas kernels  93.9 us (93%)
  local copies, waits for them, and re-layouts  3.37 us (3%)
  other arithmetic  2.04 us (2%)
    pallas_call x1, Pallas kernels, shards(): pl.pallas_call(functools.partial(kernel, n_blk, n_grp, sub, tsub, scale_x...  93.9 us

profile of v2, /device:TPU:0, one launch (start us, length us, event | category | flops | bytes accessed | tf_op | source)
XLA Modules:
  0.0 100.0 jit_solution(12302798820254993413)
XLA Ops:
  0.6 0.0 copy-start
  0.6 0.7 convert_bitcast_fusion
  1.3 0.0 copy-done
  1.3 0.0 copy-start.2
  1.3 0.0 copy-start.5
  1.3 0.0 copy-start.6
  1.4 0.7 copy-done.2
  2.0 0.0 copy-done.5
  2.0 0.0 copy-done.6
  2.0 0.1 add_multiply_fusion.1
  2.1 0.0 copy-start.1
  2.1 0.6 pad_maximum_fusion.1.tgt_ref
  2.7 0.1 copy-done.1
  2.8 0.1 add_multiply_fusion
  2.9 0.6 pad_maximum_fusion.own_ref
  3.5 93.9 %shard_map.85 = (f32[16,128]{1,0:T(8,128)}, f32[16,128]{1,0:T(8,128)}, f32[8,128]{1,0:T(8,128)}) custom-call(f32[32,128]{1,0:T(8,128)} %pad_maximum_fusion.own_ref, f32[16,128]{1,0:T(8,128)} %pad_maximum_fusion.1.tgt_ref), custom_call_target="tpu_custom_call" | custom-call | tf_op jit(solution)/shard_map/pallas_call | solution.py:402
  97.4 0.0 copy-start.4
  97.4 0.7 copy-done.4
  98.1 0.0 copy-start.7
  98.1 0.0 copy-start.3
  98.1 0.6 reshape.28
  98.7 0.1 copy-done.7
  98.8 0.6 slice.10
  99.4 0.0 copy-done.3
  99.4 0.6 reshape.29
  (4 shorter events, 0.0 us)
Async XLA Ops:
  0.6 0.7 copy-start
  1.3 0.7 copy-start.2
  1.3 0.7 copy-start.5
  1.3 0.7 copy-start.6
  2.1 0.7 copy-start.1
  97.4 0.7 copy-start.4
  98.1 0.7 copy-start.7
  98.1 1.3 %copy-start.3 = (f32[16,128]{1,0:T(8,128)S(1)}, f32[16,128]{1,0:T(8,128)}, u32[]{:S(2)}) copy-start(f32[16,128]{1,0:T(8,128)} %get-tuple-element.8) | copy-start | bytes 24580

commit v3 on v2

--- a/solution.py
+++ b/solution.py
@@ -120,28 +120,41 @@
     send0[31:32] = row0
     pl.semaphore_wait(barrier, peers - 1)
 
-    def copy_to(r, p):
-        tb, tg, e = target(p)
-        return pltpu.make_async_remote_copy(
-            src_ref=sends[r],
-            dst_ref=recvs[r].at[p],
-            send_sem=send_sem.at[r],
-            recv_sem=recv_sem.at[r],
-            device_id=(tb, tg),
-            device_id_type=MESH,
-        )
+    far_low, far_high = (wide + 1) * n_grp, (n_blk - wide) * n_grp
+    parts = ((1, far_low, False), (far_low, far_high, True), (far_high, peers, False))
+
+    def rows_of(r, far):
+        rows = recvs[r].shape[1]
+        count = min(8, rows) if far else rows
+        return pl.ds(rows - count, count)
 
     def start_round(r):
-        def body(p, carry):
-            copy_to(r, p).start()
-            return carry
-
-        lax.fori_loop(1, peers, body, 0)
+        for part, (low, high, far) in enumerate(parts):
+            rows = rows_of(r, far)
+
+            def body(p, carry, part=part, rows=rows):
+                tb, tg, e = target(p)
+                pltpu.make_async_remote_copy(
+                    src_ref=sends[r].at[rows],
+                    dst_ref=recvs[r].at[p, rows],
+                    send_sem=send_sem.at[r, part],
+                    recv_sem=recv_sem.at[r, part],
+                    device_id=(tb, tg),
+                    device_id_type=MESH,
+                ).start()
+                return carry
+
+            lax.fori_loop(low, high, body, 0)
         recvs[r][0] = sends[r][...]
 
+    def wait_bytes(r, sem):
+        for part, (low, high, far) in enumerate(parts):
+            if high > low:
+                landed = recvs[r].at[pl.ds(low, high - low), rows_of(r, far)]
+                pltpu.make_async_copy(landed, landed, sem.at[r, part]).wait()
+
     def wait_round(r):
-        landed = recvs[r].at[pl.ds(1, peers - 1)]
-        pltpu.make_async_copy(landed, landed, recv_sem.at[r]).wait()
+        wait_bytes(r, recv_sem)
         last = recvs[r].shape[1] - 1
         row = jnp.sum(recvs[r][:, last, :], axis=0, keepdims=True)
         b = jnp.broadcast_to(row, (8, LANES))
@@ -352,8 +365,7 @@
 
     lax.fori_loop(0, tsub * LANES // GROUP, tgroup, 0)
     for r in range(ITERS + 1):
-        sent = recvs[r].at[pl.ds(1, peers - 1)]
-        pltpu.make_async_copy(sent, sent, send_sem.at[r]).wait()
+        wait_bytes(r, send_sem)
     q_own = basis_rows(tgt_ref[0:tsub], tgt_ref[tsub : 2 * tsub], tgt_ref[2 * tsub : 3 * tsub])
     out_m[...] = jnp.zeros((16, LANES), jnp.float32)
     for c in range(C):
@@ -427,8 +439,8 @@
             pltpu.VMEM((near, 16, LANES), f32),
             pltpu.VMEM((near, 16, LANES), f32),
             pltpu.VMEM((near, 16, LANES), f32),
-            pltpu.SemaphoreType.DMA((4,)),
-            pltpu.SemaphoreType.DMA((4,)),
+            pltpu.SemaphoreType.DMA((4, 3)),
+            pltpu.SemaphoreType.DMA((4, 3)),
         ],
         compiler_params=pltpu.CompilerParams(
             collective_id=0, has_side_effects=True, vmem_limit_bytes=63 * 1024 * 1024

time: 101 us -> 98.1 us (0.971)
  Pallas kernels: 93.9 us -> 91.4 us
    pallas_call x1, Pallas kernels: 93.9 us -> 91.4 us  [shards(): pl.pallas_call(functools.partial(kernel, n_blk, n_grp, sub, tsub, scale_x...]
where the time goes in v3:
time: 98.1 us; the launch traced here: 97.5 us
  Pallas kernels  91.4 us (93%)
  local copies, waits for them, and re-layouts  3.37 us (3%)
  other arithmetic  2.04 us (2%)
    pallas_call x1, Pallas kernels, shards(): pl.pallas_call(functools.partial(kernel, n_blk, n_grp, sub, tsub, scale_x...  91.4 us

profile of v3, /device:TPU:0, one launch (start us, length us, event | category | flops | bytes accessed | tf_op | source)
XLA Modules:
  0.0 97.5 jit_solution(7188013846307003183)
XLA Ops:
  0.6 0.0 copy-start
  0.6 0.7 convert_bitcast_fusion
  1.3 0.0 copy-done
  1.3 0.0 copy-start.2
  1.3 0.0 copy-start.5
  1.3 0.0 copy-start.6
  1.4 0.7 copy-done.2
  2.0 0.0 copy-done.5
  2.0 0.0 copy-done.6
  2.0 0.1 add_multiply_fusion.1
  2.1 0.0 copy-start.1
  2.1 0.6 pad_maximum_fusion.1.tgt_ref
  2.7 0.1 copy-done.1
  2.8 0.1 add_multiply_fusion
  2.9 0.6 pad_maximum_fusion.own_ref
  3.5 91.4 %shard_map.85 = (f32[16,128]{1,0:T(8,128)}, f32[16,128]{1,0:T(8,128)}, f32[8,128]{1,0:T(8,128)}) custom-call(f32[32,128]{1,0:T(8,128)} %pad_maximum_fusion.own_ref, f32[16,128]{1,0:T(8,128)} %pad_maximum_fusion.1.tgt_ref), custom_call_target="tpu_custom_call" | custom-call | tf_op jit(solution)/shard_map/pallas_call | solution.py:414
  94.9 0.0 copy-start.4
  94.9 0.7 copy-done.4
  95.6 0.0 copy-start.7
  95.6 0.0 copy-start.3
  95.6 0.6 reshape.28
  96.2 0.1 copy-done.7
  96.3 0.6 slice.10
  96.9 0.0 copy-done.3
  96.9 0.6 reshape.29
  (4 shorter events, 0.0 us)
Async XLA Ops:
  0.6 0.7 copy-start
  1.3 0.7 copy-start.2
  1.3 0.7 copy-start.5
  1.3 0.7 copy-start.6
  2.1 0.7 copy-start.1
  94.9 0.7 copy-start.4
  95.6 0.7 copy-start.7
  95.6 1.3 %copy-start.3 = (f32[16,128]{1,0:T(8,128)S(1)}, f32[16,128]{1,0:T(8,128)}, u32[]{:S(2)}) copy-start(f32[16,128]{1,0:T(8,128)} %get-tuple-element.8) | copy-start | bytes 24580
